TPU v7x, 32 devices: a whole 2x2x4 slice. The times are simulated.
32 devices in a mesh: band: 16 (over z, y, core), ga: 2 (over x).
Axes of the slice: x: 2, y: 2, z: 4, core: 2. Of those that a mesh axis runs over, the one named last changes fastest.
Arguments:
- orbitals: bfloat16 [2, 16, 160, 128], P(None, 'band', 'ga'), may hold values from -8 to 8, as said below
- potential: float32 [480, 480], P('ga'), may hold values from -2 to 2
- slot_sticks: int32 [160], replicated, may hold values from -1 to 126, as said below
- stick_entries: int32 [160, 128], replicated, may hold values from -1 to 126, as said below
Outputs:
- applied_orbitals: bfloat16 [2, 16, 160, 128], P(None, 'band', 'ga')
- correlation: float32 [2, 16, 16], replicated
- reduced_hamiltonian: float32 [2, 16, 16], replicated
Inputs may be any that keep to these rules, and one draw needn't show every extreme that they name: `slot_sticks`: every gx with |gx| < 64 is held by exactly one slot; the other slots hold -1. Slots t with t // 80 = d are those of index d of ga; on some index of ga all 80 slots hold sticks. `stick_entries`: row t lists, in some order, gz + 63 for every gz with gx^2 + gz^2 < 64^2, gx being the stick of slot t, then -1 to the end of the row; rows of empty slots are all -1. `orbitals`: entries where stick_entries is -1 carry values that are not used.
All inputs are finite; a program needn't handle non-finite values.
Results may differ from a plain program's by a relative error of at most 0.001.
Values may be sent and summed in bfloat16 or wider, within the bound.
A program may use at most 64 MiB of HBM per device.

v0:
```python
import jax
import jax.numpy as jnp
from jax import lax
from jax.sharding import PartitionSpec as P

TWO_PI = 6.283185307179586
HIGHEST_PRECISION = lax.Precision.HIGHEST


def phases(frequency, position, points):
    winding = frequency[:, None] * position[None, :] % points
    angles = winding.astype(jnp.float32) * (TWO_PI / points)
    return (jnp.cos(angles), jnp.sin(angles))


def stick_phases(slot_sticks, radius, points):
    frequency = slot_sticks - radius + 1
    x_cos, x_sin = phases(frequency, jnp.arange(points, dtype=jnp.int32), points)
    filled = (slot_sticks >= 0).astype(jnp.float32)[:, None]
    return (x_cos * filled, x_sin * filled)


def selector_table(entry_lists):
    width = entry_lists.shape[1]
    return (entry_lists[:, :, None] == jnp.arange(width, dtype=jnp.int32)[None, None, :]).astype(
        jnp.bfloat16
    )


def spread_entries(coeffs, selector):
    return jnp.einsum("cbsk,skp->cbsp", coeffs, selector, preferred_element_type=jnp.float32)


def pick_entries(spectra, selector):
    return jnp.einsum(
        "cbsp,skp->cbsk", spectra, selector.astype(jnp.float32), precision=HIGHEST_PRECISION
    )


def z_forward(spread, z_cos, z_sin):
    real_part = jnp.einsum(
        "bsp,pz->bsz", spread[0], z_cos, precision=HIGHEST_PRECISION
    ) - jnp.einsum("bsp,pz->bsz", spread[1], z_sin, precision=HIGHEST_PRECISION)
    imag_part = jnp.einsum(
        "bsp,pz->bsz", spread[0], z_sin, precision=HIGHEST_PRECISION
    ) + jnp.einsum("bsp,pz->bsz", spread[1], z_cos, precision=HIGHEST_PRECISION)
    return jnp.stack([real_part, imag_part])


def plane_work(columns, x_cos, x_sin, potential):
    field_real = jnp.einsum(
        "bsz,sx->bzx", columns[0], x_cos, precision=HIGHEST_PRECISION
    ) - jnp.einsum("bsz,sx->bzx", columns[1], x_sin, precision=HIGHEST_PRECISION)
    field_imag = jnp.einsum(
        "bsz,sx->bzx", columns[0], x_sin, precision=HIGHEST_PRECISION
    ) + jnp.einsum("bsz,sx->bzx", columns[1], x_cos, precision=HIGHEST_PRECISION)
    prod_real = potential[None] * field_real
    prod_imag = potential[None] * field_imag
    back_real = jnp.einsum(
        "bzx,sx->bsz", prod_real, x_cos, precision=HIGHEST_PRECISION
    ) + jnp.einsum("bzx,sx->bsz", prod_imag, x_sin, precision=HIGHEST_PRECISION)
    back_imag = jnp.einsum(
        "bzx,sx->bsz", prod_imag, x_cos, precision=HIGHEST_PRECISION
    ) - jnp.einsum("bzx,sx->bsz", prod_real, x_sin, precision=HIGHEST_PRECISION)
    return jnp.stack([back_real, back_imag])


def z_backward(gathered, z_cos, z_sin, points):
    real_part = jnp.einsum(
        "bsz,pz->bsp", gathered[0], z_cos, precision=HIGHEST_PRECISION
    ) + jnp.einsum("bsz,pz->bsp", gathered[1], z_sin, precision=HIGHEST_PRECISION)
    imag_part = jnp.einsum(
        "bsz,pz->bsp", gathered[1], z_cos, precision=HIGHEST_PRECISION
    ) - jnp.einsum("bsz,pz->bsp", gathered[0], z_sin, precision=HIGHEST_PRECISION)
    return jnp.stack([real_part, imag_part]) / float(points * points)


def kinetic_factor(sticks, entry_lists, radius):
    gx_value = sticks - radius + 1
    gz_value = entry_lists - radius + 1
    return ((gx_value * gx_value)[:, None] + gz_value * gz_value).astype(jnp.float32) / float(
        radius * radius
    )


def cross_products(left, right, scale):
    dims = (((1,), (1,)), ((), ()))
    real_part = lax.dot_general(
        left[0], right[0], dims, preferred_element_type=jnp.float32
    ) + lax.dot_general(left[1], right[1], dims, preferred_element_type=jnp.float32)
    imag_part = lax.dot_general(
        left[0], right[1], dims, preferred_element_type=jnp.float32
    ) - lax.dot_general(left[1], right[0], dims, preferred_element_type=jnp.float32)
    return jnp.stack([real_part, imag_part]) * scale


def body(orbitals, potential, slot_sticks, stick_entries):
    points = potential.shape[1]
    width = stick_entries.shape[1]
    radius = width // 2
    band_count = orbitals.shape[1]
    slot_count = orbitals.shape[2]
    ga_index = lax.axis_index("ga")
    own_first = ga_index * slot_count
    own_lists = lax.dynamic_slice_in_dim(stick_entries, own_first, slot_count, 0)
    own_sticks = lax.dynamic_slice_in_dim(slot_sticks, own_first, slot_count, 0)
    present = own_lists >= 0
    own_selector = selector_table(own_lists)
    masked = jnp.where(present[None, None], orbitals, jnp.zeros_like(orbitals))
    frequency = jnp.arange(width, dtype=jnp.int32) - radius + 1
    whole_cos, whole_sin = phases(frequency, jnp.arange(points, dtype=jnp.int32), points)
    x_cos, x_sin = stick_phases(slot_sticks, radius, points)
    columns = z_forward(spread_entries(orbitals, own_selector), whole_cos, whole_sin)
    planes_columns = lax.all_to_all(columns, "ga", split_axis=3, concat_axis=2, tiled=True)
    gathered = plane_work(planes_columns, x_cos, x_sin, potential)
    returned = lax.all_to_all(gathered, "ga", split_axis=2, concat_axis=3, tiled=True)
    spectra = z_backward(returned, whole_cos, whole_sin, points)
    applied = pick_entries(spectra, own_selector)
    kinetic = kinetic_factor(own_sticks, own_lists, radius)
    applied_orbitals = jnp.where(
        present[None, None],
        kinetic[None, None] * orbitals.astype(jnp.float32) + applied,
        jnp.float32(0.0),
    ).astype(jnp.bfloat16)
    scale = 1.0 / (4.0 * radius * radius)
    flat_psi = masked.reshape(2, band_count, -1)
    flat_h = applied_orbitals.reshape(2, band_count, -1)
    portion = lax.all_gather(masked, "band", axis=1, tiled=True)
    remote_psi = portion.reshape(2, portion.shape[1], -1)
    block = jnp.stack(
        [cross_products(remote_psi, flat_psi, scale), cross_products(remote_psi, flat_h, scale)]
    )
    summed = lax.psum(block, "ga")
    matrices = lax.all_gather(summed, "band", axis=3, tiled=True)
    return (applied_orbitals, matrices[0], matrices[1])


def solution(mesh):
    return jax.shard_map(
        body,
        mesh=mesh,
        in_specs=(P(None, "band", "ga", None), P("ga", None), P(), P()),
        out_specs=(P(None, "band", "ga", None), P(), P()),
        check_vma=False,
    )
```

profile of v0, /device:TPU:0, one launch (start us, length us, event | category | flops | bytes accessed | tf_op | source)
XLA Modules:
  0.0 106.6 jit_solution(10663238395581667539)
XLA Ops:
  2.3 3.0 %fusion.10 = f32[2,1,80,128]{3,0,2,1:T(2,128)S(1)} fusion(s32[80,128]{1,0:T(8,128)S(1)} %get-tuple-element.16, bf16[2,80,128]{2,1,0:T(8,128)(2,1)} %bitcast.158), kind=kOutput, calls=%fused_computation.17 | convolution fusion | flops 6553600 | bytes 163840 | tf_op jit(solution)/shard_map/cbsk,skp->cbsp/dot_general | solution.py:31
  5.3 1.3 %fusion.53 = f32[80,480]{1,0:T(8,128)S(1)} fusion(f32[80,128]{1,0:T(8,128)S(1)} %bitcast.156, s32[128]{0:T(128)S(1)} %iota_add_fusion), kind=kOutput, calls=%fused_computation.76 | convolution fusion | flops 59535360 | bytes 195072 | tf_op jit(solution)/shard_map/bsp,pz->bsz/dot_general | solution.py:41
  6.7 1.4 %fusion.57 = f32[80,480]{1,0:T(8,128)S(1)} fusion(f32[80,128]{1,0:T(8,128)S(1)} %bitcast.157, s32[128]{0:T(128)S(1)} %iota_add_fusion), kind=kOutput, calls=%fused_computation.77 | convolution fusion | flops 59535360 | bytes 195072 | tf_op jit(solution)/shard_map/bsp,pz->bsz/dot_general | solution.py:44
  8.1 1.4 %fusion.9 = f32[1,1,80,480]{3,2,1,0:T(8,128)S(1)} fusion(f32[80,480]{1,0:T(8,128)S(1)} %fusion.53, f32[80,128]{1,0:T(8,128)S(1)} %bitcast.154, s32[128]{0:T(128)S(1)} %iota_add_fusion), kind=kOutput, calls=%fused_computation.16 | convolution fusion | flops 59573760 | bytes 348672 | tf_op jit(solution)/shard_map/bsp,pz->bsz/dot_general | solution.py:43
  9.5 1.4 %fusion.8 = f32[1,1,80,480]{3,2,1,0:T(8,128)S(1)} fusion(f32[80,480]{1,0:T(8,128)S(1)} %fusion.57, f32[80,128]{1,0:T(8,128)S(1)} %bitcast.155, s32[128]{0:T(128)S(1)} %iota_add_fusion), kind=kOutput, calls=%fused_computation.14 | convolution fusion | flops 59573760 | bytes 348672 | tf_op jit(solution)/shard_map/bsp,pz->bsz/dot_general | solution.py:46
  11.9 4.4 %all-to-all-start = ((f32[2,1,80,480]{2,1,0,3:T(1,128)}), f32[2,1,80,480]{2,1,0,3:T(1,128)S(1)}, u32[]{:S(2)}, u32[]{:S(2)}) async-start(f32[2,1,80,480]{2,1,0,3:T(1,128)} %copy.37), calls=%async_computation | async-start | bytes 983040 | tf_op jit(solution)/shard_map/all_to_all | solution.py:114
  16.4 24.4 %all_gather.6 = bf16[2,16,80,128]{3,2,0,1:T(8,128)(2,1)S(1)} all-gather(bf16[2,1,80,128]{3,2,0,1:T(8,128)(2,1)S(1)} %copy.45), channel_id=1, replica_groups=mesh['band'=16,'ga'=2] {'band'}, dimensions={1}, use_global_device_ids=true | all-gather | bytes 696320 | tf_op jit(solution)/shard_map/all_gather | solution.py:128
  42.3 1.9 %fusion.40 = f32[240,480]{1,0:T(8,128)S(1)} fusion(f32[160,240]{1,0:T(8,128)S(1)} %bitcast.152, f32[160]{0:T(256)S(1)} %compare_convert_fusion, s32[160]{0:T(256)S(1)} %broadcast_add_fusion), kind=kOutput, calls=%fused_computation.65 | convolution fusion | flops 221952000 | bytes 615680 | tf_op jit(solution)/shard_map/bsz,sx->bzx/dot_general | solution.py:51
  44.2 1.9 %fusion.41 = f32[240,480]{1,0:T(8,128)S(1)} fusion(f32[160,240]{1,0:T(8,128)S(1)} %bitcast.153, f32[160]{0:T(256)S(1)} %compare_convert_fusion, s32[160]{0:T(256)S(1)} %broadcast_add_fusion), kind=kOutput, calls=%fused_computation.66 | convolution fusion | flops 221952000 | bytes 615680 | tf_op jit(solution)/shard_map/bsz,sx->bzx/dot_general | solution.py:54
  46.1 1.9 %fusion.5 = f32[240,480]{1,0:T(8,128)S(1)} fusion(f32[240,480]{1,0:T(8,128)S(1)} %copy-done, f32[240,480]{1,0:T(8,128)S(1)} %fusion.40, f32[160,240]{1,0:T(8,128)S(1)} %bitcast.139, f32[160]{0:T(256)S(1)} %compare_convert_fusion, s32[160]{0:T(256)S(1)} %broadcast_add_fusion), kind=kOutput, calls=%fused_computation.8 | convolution fusion | flops 222182400 | bytes 1537280 | tf_op jit(solution)/shard_map/bsz,sx->bzx/dot_general | solution.py:53
  48.0 1.9 %fusion.39 = f32[160,240]{1,0:T(8,128)S(1)} fusion(f32[240,480]{1,0:T(8,128)S(1)} %fusion.5, f32[160]{0:T(256)S(1)} %compare_convert_fusion, s32[160]{0:T(256)S(1)} %broadcast_add_fusion), kind=kOutput, calls=%fused_computation.64 | convolution fusion | flops 221952000 | bytes 615680 | tf_op jit(solution)/shard_map/bzx,sx->bsz/dot_general | solution.py:59
  49.9 1.9 %fusion.4 = f32[240,480]{1,0:T(8,128)S(1)} fusion(f32[240,480]{1,0:T(8,128)S(1)} %copy-done, f32[240,480]{1,0:T(8,128)S(1)} %fusion.41, f32[160,240]{1,0:T(8,128)S(1)} %bitcast.140, f32[160]{0:T(256)S(1)} %compare_convert_fusion, s32[160]{0:T(256)S(1)} %broadcast_add_fusion), kind=kOutput, calls=%fused_computation.6 | convolution fusion | flops 222182400 | bytes 1537280 | tf_op jit(solution)/shard_map/bsz,sx->bzx/dot_general | solution.py:56
  51.8 1.9 %fusion.38 = f32[160,240]{1,0:T(8,128)S(1)} fusion(f32[240,480]{1,0:T(8,128)S(1)} %fusion.4, f32[160]{0:T(256)S(1)} %compare_convert_fusion, s32[160]{0:T(256)S(1)} %broadcast_add_fusion), kind=kOutput, calls=%fused_computation.63 | convolution fusion | flops 221952000 | bytes 615680 | tf_op jit(solution)/shard_map/bzx,sx->bsz/dot_general | solution.py:62
  53.7 2.1 %fusion.7 = f32[1,1,160,240]{3,2,1,0:T(8,128)S(1)} fusion(f32[160,240]{1,0:T(8,128)S(1)} %fusion.39, f32[240,480]{1,0:T(8,128)S(1)} %fusion.4, f32[160]{0:T(256)S(1)} %compare_convert_fusion, s32[160]{0:T(256)S(1)} %broadcast_add_fusion), kind=kOutput, calls=%fused_computation.12 | convolution fusion | flops 221990400 | bytes 769280 | tf_op jit(solution)/shard_map/bzx,sx->bsz/dot_general | solution.py:61
  55.9 1.9 %fusion.6 = f32[1,1,160,240]{3,2,1,0:T(8,128)S(1)} fusion(f32[160,240]{1,0:T(8,128)S(1)} %fusion.38, f32[240,480]{1,0:T(8,128)S(1)} %fusion.5, f32[160]{0:T(256)S(1)} %compare_convert_fusion, s32[160]{0:T(256)S(1)} %broadcast_add_fusion), kind=kOutput, calls=%fused_computation.10 | convolution fusion | flops 221990400 | bytes 769280 | tf_op jit(solution)/shard_map/bzx,sx->bsz/dot_general | solution.py:64
  58.9 3.5 %all-to-all-start.1 = ((f32[2,1,160,240]{3,1,0,2:T(1,128)}), f32[2,1,160,240]{3,1,0,2:T(1,128)S(1)}, u32[]{:S(2)}, u32[]{:S(2)}) async-start(f32[2,1,160,240]{3,1,0,2:T(1,128)} %copy.41), calls=%async_computation.1 | async-start | bytes 655360 | tf_op jit(solution)/shard_map/all_to_all | solution.py:116
  62.8 6.5 %all-to-all-done.1 = f32[2,1,160,240]{3,1,0,2:T(1,128)S(1)} async-done(((f32[2,1,160,240]{3,1,0,2:T(1,128)}), f32[2,1,160,240]{3,1,0,2:T(1,128)S(1)}, u32[]{:S(2)}, u32[]{:S(2)}) %all-to-all-start.1) | async-done | bytes 307232 | tf_op jit(solution)/shard_map/all_to_all | solution.py:116
  70.0 1.4 %fusion.50 = f32[80,128]{1,0:T(8,128)S(1)} fusion(f32[80,480]{1,0:T(8,128)S(1)} %reshape.267, s32[128]{0:T(128)S(1)} %iota_add_fusion), kind=kOutput, calls=%fused_computation.75 | convolution fusion | flops 59535360 | bytes 195072 | tf_op jit(solution)/shard_map/bsz,pz->bsp/dot_general | solution.py:69
  71.6 1.4 %fusion.48 = f32[80,128]{1,0:T(8,128)S(1)} fusion(f32[80,480]{1,0:T(8,128)S(1)} %reshape.268, s32[128]{0:T(128)S(1)} %iota_add_fusion), kind=kOutput, calls=%fused_computation.74 | convolution fusion | flops 59535360 | bytes 195072 | tf_op jit(solution)/shard_map/bsz,pz->bsp/dot_general | solution.py:72
  73.0 1.4 %fusion.16 = f32[1,80,128]{2,1,0:T(8,128)S(1)} fusion(f32[80,128]{1,0:T(8,128)S(1)} %fusion.50, f32[80,480]{1,0:T(8,128)S(1)} %reshape.268, s32[128]{0:T(128)S(1)} %iota_add_fusion), kind=kOutput, calls=%fused_computation.25 | convolution fusion | flops 59545600 | bytes 236032 | tf_op jit(solution)/shard_map/bsz,pz->bsp/dot_general | solution.py:71
  74.5 1.5 %fusion.15 = f32[1,80,128]{2,1,0:T(8,128)S(1)} fusion(f32[80,128]{1,0:T(8,128)S(1)} %fusion.48, f32[80,480]{1,0:T(8,128)S(1)} %reshape.267, s32[128]{0:T(128)S(1)} %iota_add_fusion), kind=kOutput, calls=%fused_computation.23 | convolution fusion | flops 59545600 | bytes 236032 | tf_op jit(solution)/shard_map/bsz,pz->bsp/dot_general | solution.py:74
  76.0 5.6 %fusion.14 = bf16[2,1,80,128]{3,0,2,1:T(2,128)(2,1)S(1)} fusion(s32[80,128]{1,0:T(8,128)S(1)} %get-tuple-element.16, f32[2,80,128]{2,1,0:T(8,128)S(1)} %maximum_multiply_fusion, pred[80,128]{1,0:T(8,128)(4,1)S(1)} %broadcast_compare_fusion, f32[80,128]{1,0:T(8,128)S(1)} %get-tuple-element.15, bf16[2,1,80,128]{3,2,1,0:T(8,128)(2,1)S(1)} %copy-done.1), kind=kOutput, calls=%fused_computation.21 | convolution fusion | flops 32870400 | bytes 256000 | tf_op jit(solution)/shard_map/cbsp,skp->cbsk/dot_general | solution.py:35
  83.1 4.9 %psum.7 = f32[2,2,16,1]{2,3,1,0:T(1,128)S(1)} all-reduce(f32[2,2,16,1]{2,3,1,0:T(1,128)S(1)} %pad_maximum_fusion.2), channel_id=1, replica_groups=mesh['band'=16,'ga'=2] {'ga'}, use_global_device_ids=true, to_apply=%region_0.1 | all-reduce | flops 64 | bytes 512 | tf_op jit(solution)/shard_map/psum | solution.py:133
  88.1 17.2 %all_gather.7 = f32[2,2,16,16]{2,1,0,3:T(2,128)S(1)} all-gather(f32[2,2,16,1]{2,1,0,3:T(2,128)S(1)} %bitcast.159), channel_id=1, replica_groups=mesh['band'=16,'ga'=2] {'band'}, dimensions={3}, use_global_device_ids=true | all-gather | bytes 4352 | tf_op jit(solution)/shard_map/all_gather | solution.py:134
  (45 shorter events, 9.7 us)
Async XLA Ops:
  11.9 4.4 %copy-start.2 = (s32[160]{0:T(256)S(1)}, s32[160]{0:T(256)}, u32[]{:S(2)}) copy-start(s32[160]{0:T(256)} %param.6) | copy-start | bytes 1924
  11.9 4.4 %copy-start.1 = (bf16[2,1,80,128]{3,2,1,0:T(8,128)(2,1)S(1)}, bf16[2,1,80,128]{3,2,1,0:T(8,128)(2,1)}, u32[]{:S(2)}) copy-start(bf16[2,1,80,128]{3,2,1,0:T(8,128)(2,1)} %param.4) | copy-start | bytes 122884
  11.9 29.4 %all-to-all-start = ((f32[2,1,80,480]{2,1,0,3:T(1,128)}), f32[2,1,80,480]{2,1,0,3:T(1,128)S(1)}, u32[]{:S(2)}, u32[]{:S(2)}) async-start(f32[2,1,80,480]{2,1,0,3:T(1,128)} %copy.37), calls=%async_computation | async-start | bytes 983040 | tf_op jit(solution)/shard_map/all_to_all | solution.py:114
  44.2 1.9 %copy-start = (f32[240,480]{1,0:T(8,128)S(1)}, f32[240,480]{1,0:T(8,128)}, u32[]{:S(2)}) copy-start(f32[240,480]{1,0:T(8,128)} %param.5) | copy-start | bytes 1382404
  58.9 10.4 %all-to-all-start.1 = ((f32[2,1,160,240]{3,1,0,2:T(1,128)}), f32[2,1,160,240]{3,1,0,2:T(1,128)S(1)}, u32[]{:S(2)}, u32[]{:S(2)}) async-start(f32[2,1,160,240]{3,1,0,2:T(1,128)} %copy.41), calls=%async_computation.1 | async-start | bytes 655360 | tf_op jit(solution)/shard_map/all_to_all | solution.py:116
where the time goes:
time: 107 us
  blocking collectives  46.5 us (43%)
  matrix products  37 us (35%)
  starting transfers between devices  7.82 us (7%)
  waiting for transfers between devices  6.46 us (6%)
  local copies, waits for them, and re-layouts  6.1 us (6%)
  other arithmetic  1.8 us (2%)
    all_gather x1, blocking collectives, body(): portion = lax.all_gather(masked, 'band', axis=1, tiled=True)  24.4 us
    all_gather x1, blocking collectives, body(): matrices = lax.all_gather(summed, 'band', axis=3, tiled=True)  17.2 us
    all_to_all x1, waiting for transfers between devices, body(): lax.all_to_all(gathered, 'ga', split_axis=2, concat_axis=3, tiled=True)  6.46 us
    dot_general x1, matrix products, pick_entries(): jnp.einsum('cbsp,skp->cbsk', spectra, selector.astype(jnp.float32), preci...  5.62 us
    psum x1, blocking collectives, body(): summed = lax.psum(block, 'ga')  4.93 us
    all_to_all x1, starting transfers between devices, body(): lax.all_to_all(columns, 'ga', split_axis=3, concat_axis=2, tiled=True)  4.36 us
    all_to_all x1, starting transfers between devices, body(): lax.all_to_all(gathered, 'ga', split_axis=2, concat_axis=3, tiled=True)  3.45 us
    dot_general x1, matrix products, spread_entries(): jnp.einsum('cbsk,skp->cbsp', coeffs, selector, preferred_element_type=jnp...  3.01 us
  transfers between devices with their start and end apart: 2, of which 1 were waited for; matrix products, arithmetic and copies ran while one was open for 1% of the time, Pallas kernels for 0%

commit v1 on v0

v1 whole, which is shorter than its diff:
```python
import functools

import jax
import jax.numpy as jnp
import numpy as np
from jax import lax
from jax.experimental import pallas as pl
from jax.experimental.pallas import tpu as pltpu
from jax.sharding import PartitionSpec as P

MESH = pl.DeviceIdType.MESH
NT = (((1,), (1,)), ((), ()))
BF16 = jnp.bfloat16
F32 = jnp.float32


def split_np(table):
    high = table.astype(np.float32).astype(BF16)
    low = (table - high.astype(np.float64)).astype(np.float32).astype(BF16)
    return np.stack([high, low])


def tables(points, width, radius, groups, planes, plane_pad, coarse):
    freq = np.arange(width) - radius + 1
    used = (np.arange(width) < width - 1).astype(np.float64)
    z_tabs = []
    for group in range(groups):
        z = np.arange(planes) + group * planes
        angle = 2.0 * np.pi * ((freq[:, None] * z[None, :]) % points) / points
        cos = np.zeros((width, plane_pad))
        sin = np.zeros((width, plane_pad))
        cos[:, :planes] = np.cos(angle) * used[:, None]
        sin[:, :planes] = np.sin(angle) * used[:, None]
        z_tabs.append(split_np(np.block([[cos, sin], [-sin, cos]])))
    x = np.arange(coarse)
    angle = 2.0 * np.pi * ((freq[None, :] * x[:, None]) % coarse) / coarse
    cos = np.cos(angle) * used[None, :]
    sin = np.sin(angle) * used[None, :]
    forward = np.block([[cos, -sin], [sin, cos]])
    limit = 2 * (radius - 1)
    offset = (x[:, None] * points - np.arange(points)[None, :] * coarse) % (coarse * points)
    base = 2.0 * np.pi * offset / (coarse * points)
    resample = np.ones((coarse, points))
    for g in range(1, limit + 1):
        resample += 2.0 * np.cos(g * base)
    resample /= points
    return (
        np.stack(z_tabs),
        split_np(forward),
        split_np(forward.T.copy()),
        split_np(resample),
    )


def split(value):
    high = value.astype(BF16)
    low = (value - high.astype(F32)).astype(BF16)
    return high, low


def dot(a, b):
    return jnp.dot(a, b, preferred_element_type=F32)


def dot_nt(a, b):
    return lax.dot_general(a, b, NT, preferred_element_type=F32)


def take_lanes(value, index):
    return jnp.take_along_axis(value, index, axis=1, mode="promise_in_bounds")


def kernel(
    bands,
    groups,
    points,
    radius,
    orb_ref,
    slots_ref,
    entries_ref,
    pot_hbm,
    tz_hbm,
    tx_hbm,
    ty_hbm,
    tr_hbm,
    out_ref,
    corr_ref,
    red_ref,
    tz,
    tx,
    ty,
    tr,
    pot,
    spread,
    colbuf,
    part,
    got,
    gather,
    sums,
    message,
    inbox,
    load_sem,
    s_send,
    s_recv,
    p_send,
    p_recv,
    g_send,
    g_recv,
    m_send,
    m_recv,
):
    band = lax.axis_index("band")
    ga = lax.axis_index("ga")
    total = bands * groups
    me = ga * bands + band
    slots = orb_ref.shape[2]
    width = orb_ref.shape[3]
    planes = pot_hbm.shape[0]
    plane_pad = pot.shape[0]
    coarse = ty.shape[2] // 2
    msg_width = message.shape[1]

    def where_is(index):
        return (lax.rem(index, bands), lax.div(index, bands))

    barrier = pltpu.get_barrier_semaphore()

    @pl.loop(1, total)
    def _(k):
        pl.semaphore_signal(
            barrier, inc=1, device_id=where_is(lax.rem(me + k, total)), device_id_type=MESH
        )

    loads = [
        pltpu.make_async_copy(pot_hbm, pot.at[pl.ds(0, planes)], load_sem.at[0]),
        pltpu.make_async_copy(tr_hbm, tr, load_sem.at[1]),
        pltpu.make_async_copy(tz_hbm.at[ga], tz, load_sem.at[2]),
        pltpu.make_async_copy(tx_hbm, tx, load_sem.at[3]),
        pltpu.make_async_copy(ty_hbm, ty, load_sem.at[4]),
    ]
    for load in loads:
        load.start()
    if plane_pad > planes:
        pot[pl.ds(planes, plane_pad - planes), :] = jnp.zeros(
            (plane_pad - planes, pot.shape[1]), F32
        )

    sums[...] = jnp.zeros_like(sums)

    own = entries_ref[pl.ds(pl.multiple_of(ga * slots, 8), slots), :]
    lane = lax.broadcasted_iota(jnp.int32, (slots, width), 1)
    inverse = jnp.full((slots, width), -1, jnp.int32)
    for k in range(width):
        inverse = jnp.where(own[:, k : k + 1] == lane, k, inverse)
    re = orb_ref[0, 0].astype(F32)
    im = orb_ref[1, 0].astype(F32)
    filled = inverse >= 0
    index = jnp.maximum(inverse, 0)
    spread[ga, :, :width] = jnp.where(filled, take_lanes(re, index), 0.0).astype(BF16)
    spread[ga, :, width:] = jnp.where(filled, take_lanes(im, index), 0.0).astype(BF16)

    pl.semaphore_wait(barrier, total - 1)

    s_copies = []
    for k in range(1, groups):
        copy = pltpu.make_async_remote_copy(
            src_ref=spread.at[ga],
            dst_ref=spread.at[ga],
            send_sem=s_send.at[k - 1],
            recv_sem=s_recv.at[k - 1],
            device_id=(band, lax.rem(ga + k, groups)),
            device_id_type=MESH,
        )
        copy.start()
        s_copies.append(copy)

    def gather_copy(k):
        return pltpu.make_async_remote_copy(
            src_ref=orb_ref.at[:, 0],
            dst_ref=gather.at[band],
            send_sem=g_send.at[k],
            recv_sem=g_recv.at[k],
            device_id=(lax.rem(band + k, bands), ga),
            device_id_type=MESH,
        )

    @pl.loop(1, bands)
    def _(k):
        gather_copy(k).start()

    loads[0].wait()
    loads[1].wait()
    pot_hi, pot_lo = split(pot[...])
    weight = dot_nt(tr[0], pot_hi) + dot_nt(tr[0], pot_lo) + dot_nt(tr[1], pot_hi)

    for copy in s_copies:
        copy.wait()
    dense = jnp.zeros((width, 2 * width), F32)
    sub = lax.broadcasted_iota(jnp.int32, (width, slots), 0)
    for g in range(groups):
        choose = jnp.where(sub == slots_ref[g : g + 1, :], 1.0, 0.0).astype(BF16)
        dense += dot(choose, spread[g])
    dense = dense.astype(BF16)

    loads[2].wait()
    columns = dot(dense, tz[0]) + dot(dense, tz[1])
    col_hi, col_lo = split(columns)
    colbuf[0, :width] = col_hi[:, :plane_pad]
    colbuf[0, width:] = col_hi[:, plane_pad:]
    colbuf[1, :width] = col_lo[:, :plane_pad]
    colbuf[1, width:] = col_lo[:, plane_pad:]
    loads[3].wait()
    field = dot(tx[0], colbuf[0]) + dot(tx[0], colbuf[1]) + dot(tx[1], colbuf[0])
    product = jnp.concatenate([field[:coarse] * weight, field[coarse:] * weight], axis=0)
    pro_hi, pro_lo = split(product)
    loads[4].wait()
    back = dot(ty[0], pro_hi) + dot(ty[0], pro_lo) + dot(ty[1], pro_hi)
    back = jnp.concatenate([back[:width], back[width:]], axis=1)
    back_hi, back_lo = split(back)
    spectra = dot_nt(back_hi, tz[0]) + dot_nt(back_hi, tz[1]) + dot_nt(back_lo, tz[0])
    spectra = spectra * (1.0 / float(points * coarse))
    spec_hi, spec_lo = split(spectra)

    eye = lax.broadcasted_iota(jnp.int32, (slots, slots), 0) == lax.broadcasted_iota(
        jnp.int32, (slots, slots), 1
    )

    def stick_column(g):
        row = slots_ref[pl.ds(g, 1), :].astype(F32)
        return jnp.sum(jnp.where(eye, row, 0.0), axis=1, keepdims=True)

    lane_f = lane.astype(F32)
    p_copies = []
    for k in range(1, groups + 1):
        target = lax.rem(ga + k, groups)
        stick = stick_column(target)
        choose = jnp.where(stick == lane_f, 1.0, 0.0).astype(BF16)
        mine = dot(choose, spec_hi) + dot(choose, spec_lo)
        if k < groups:
            part[k - 1] = mine
            copy = pltpu.make_async_remote_copy(
                src_ref=part.at[k - 1],
                dst_ref=got.at[k - 1],
                send_sem=p_send.at[k - 1],
                recv_sem=p_recv.at[k - 1],
                device_id=(band, target),
                device_id_type=MESH,
            )
            copy.start()
            p_copies.append(copy)

    present = own >= 0
    gx = stick - float(radius - 1)
    gz = (own - (radius - 1)).astype(F32)
    kinetic = (gx * gx + gz * gz) * (1.0 / float(radius * radius))
    own_index = jnp.maximum(own, 0)

    gather[band] = orb_ref[:, 0]

    @pl.loop(1, bands)
    def _(k):
        gather_copy(k).wait()

    m_re = jnp.where(present, re, 0.0)
    m_im = jnp.where(present, im, 0.0)

    def add_products(first, right_re, right_im):
        @pl.loop(0, bands)
        def _(b):
            left_re = gather[b, 0].astype(F32)
            left_im = gather[b, 1].astype(F32)
            real = left_re * right_re + left_im * right_im
            imag = left_re * right_im - left_im * right_re
            sums[pl.ds(first * bands + b, 1), :] = jnp.sum(real, axis=0, keepdims=True)
            sums[pl.ds((first + 1) * bands + b, 1), :] = jnp.sum(imag, axis=0, keepdims=True)

    add_products(0, m_re, m_im)

    for copy in p_copies:
        copy.wait()
    for k in range(1, groups):
        mine += got[k - 1]
    a_re = take_lanes(mine[:, :width], own_index)
    a_im = take_lanes(mine[:, width:], own_index)
    h_re = jnp.where(present, kinetic * re + a_re, 0.0).astype(BF16)
    h_im = jnp.where(present, kinetic * im + a_im, 0.0).astype(BF16)
    out_ref[0, 0] = h_re
    out_ref[1, 0] = h_im
    add_products(2, h_re.astype(F32), h_im.astype(F32))

    ones = jnp.full((8, width), 1.0 / float(4 * radius * radius), F32)
    row = lax.dot_general(
        ones, sums[...], NT, preferred_element_type=F32, precision=lax.Precision.HIGHEST
    )
    message[...] = row[:1]
    inbox[pl.ds(me, 1), 0, :] = row[:1]

    @pl.loop(1, total)
    def _(k):
        pltpu.make_async_remote_copy(
            src_ref=message,
            dst_ref=inbox.at[me],
            send_sem=m_send,
            recv_sem=m_recv,
            device_id=where_is(lax.rem(me + k, total)),
            device_id_type=MESH,
        ).start()

    everyone = inbox.at[pl.ds(0, total - 1)]
    pltpu.make_async_copy(everyone, everyone, m_recv).wait()
    pltpu.make_async_copy(everyone, everyone, m_send).wait()

    rows = inbox[0:bands, 0, :]
    for g in range(1, groups):
        rows += inbox[g * bands : (g + 1) * bands, 0, :]
    unit = (
        lax.broadcasted_iota(jnp.int32, (msg_width, msg_width), 0)
        == lax.broadcasted_iota(jnp.int32, (msg_width, msg_width), 1)
    ).astype(F32)
    turned = lax.dot_general(
        unit, rows, NT, preferred_element_type=F32, precision=lax.Precision.HIGHEST
    )
    for c in range(2):
        corr_ref[c] = turned[c * bands : (c + 1) * bands]
        red_ref[c] = turned[(c + 2) * bands : (c + 3) * bands]


def body(bands, groups, orbitals, potential, slot_sticks, stick_entries):
    points = potential.shape[1]
    planes = potential.shape[0]
    width = stick_entries.shape[1]
    radius = width // 2
    slots = orbitals.shape[2]
    plane_pad = -(-planes // 128) * 128
    coarse = 2 * width
    sum_rows = -(-4 * bands // 128) * 128
    tz, tx, ty, tr = tables(points, width, radius, groups, planes, plane_pad, coarse)
    vmem = pl.BlockSpec(memory_space=pltpu.VMEM)
    hbm = pl.BlockSpec(memory_space=pl.ANY)
    total = bands * groups
    dma = pltpu.SemaphoreType.DMA
    return pl.pallas_call(
        functools.partial(kernel, bands, groups, points, radius),
        out_shape=(
            jax.ShapeDtypeStruct(orbitals.shape, BF16),
            jax.ShapeDtypeStruct((2, bands, bands), F32),
            jax.ShapeDtypeStruct((2, bands, bands), F32),
        ),
        in_specs=[vmem, vmem, vmem, hbm, hbm, hbm, hbm, hbm],
        out_specs=(vmem, vmem, vmem),
        scratch_shapes=[
            pltpu.VMEM(tz.shape[1:], BF16),
            pltpu.VMEM(tx.shape, BF16),
            pltpu.VMEM(ty.shape, BF16),
            pltpu.VMEM(tr.shape, BF16),
            pltpu.VMEM((plane_pad, points), F32),
            pltpu.VMEM((groups, slots, 2 * width), BF16),
            pltpu.VMEM((2, 2 * width, plane_pad), BF16),
            pltpu.VMEM((groups - 1, slots, 2 * width), F32),
            pltpu.VMEM((groups - 1, slots, 2 * width), F32),
            pltpu.VMEM((bands, 2, slots, width), BF16),
            pltpu.VMEM((sum_rows, width), F32),
            pltpu.VMEM((1, sum_rows), F32),
            pltpu.VMEM((total, 1, sum_rows), F32),
            dma((5,)),
            dma((groups - 1,)),
            dma((groups - 1,)),
            dma((groups - 1,)),
            dma((groups - 1,)),
            dma((bands,)),
            dma((bands,)),
            dma,
            dma,
        ],
        compiler_params=pltpu.CompilerParams(
            collective_id=0, has_side_effects=True, vmem_limit_bytes=48 * 1024 * 1024
        ),
    )(orbitals, slot_sticks.reshape(groups, slots), stick_entries, potential, tz, tx, ty, tr)


def solution(mesh):
    bands = mesh.shape["band"]
    groups = mesh.shape["ga"]
    return jax.shard_map(
        functools.partial(body, bands, groups),
        mesh=mesh,
        in_specs=(P(None, "band", "ga", None), P("ga", None), P(), P()),
        out_specs=(P(None, "band", "ga", None), P(), P()),
        check_vma=False,
    )
```

time: 107 us -> 39.9 us (0.37)
  blocking collectives: 46.5 us -> 0 us
  matrix products: 37 us -> 0 us
  Pallas kernels: 0 us -> 29.1 us
  starting transfers between devices: 7.82 us -> 0 us
  waiting for transfers between devices: 6.46 us -> 0 us
  local copies, waits for them, and re-layouts: 6.1 us -> 9.63 us
  other arithmetic: 1.8 us -> 0 us
    all_gather x2 -> x0, blocking collectives: 41.6 us -> none  [the longest x1 24.4 us: body(): portion = lax.all_gather(masked, 'band', axis=1, tiled=True)]
    dot_general x26 -> x0, matrix products: 37 us -> none  [the longest x1 5.62 us: pick_entries(): jnp.einsum('cbsp,skp->cbsk', spectra, selector.astype(jnp.float32), preci...]
    pallas_call x0 -> x1, Pallas kernels: none -> 29.1 us  [body(): pl.pallas_call(functools.partial(kernel, bands, groups, points, radius),...]
    all_to_all x2 -> x0, starting transfers between devices: 7.82 us -> none  [the longest x1 4.36 us: body(): lax.all_to_all(columns, 'ga', split_axis=3, concat_axis=2, tiled=True)]
    unnamed x10 -> x17, local copies, waits for them, and re-layouts: 2.18 us -> 8.87 us
    all_to_all x2 -> x0, waiting for transfers between devices: 6.46 us -> none  [the longest x1 6.46 us: body(): lax.all_to_all(gathered, 'ga', split_axis=2, concat_axis=3, tiled=True)]
    psum x1 -> x0, blocking collectives: 4.93 us -> none  [body(): summed = lax.psum(block, 'ga')]
    another operation x4 -> x0, local copies, waits for them, and re-layouts: 2.44 us -> none  [the longest x1 1.06 us: plane_work(): return jnp.stack([back_real, back_imag])]
  transfers between devices with their start and end apart: 2 -> 0, of which waited for: 1 -> 0; matrix products, arithmetic and copies ran while one was open for 1% -> 0% of each run, Pallas kernels for 0% -> 0%
where the time goes in v1:
time: 39.9 us; the launch traced here: 39.4 us
  Pallas kernels  29.1 us (73%)
  local copies, waits for them, and re-layouts  9.63 us (24%)
  between operations  0.65 us (2%)
    pallas_call x1, Pallas kernels, body(): pl.pallas_call(functools.partial(kernel, bands, groups, points, radius),...  29.1 us
    unnamed x17, local copies, waits for them, and re-layouts  8.87 us

profile of v1, /device:TPU:0, one launch (start us, length us, event | category | flops | bytes accessed | tf_op | source)
XLA Modules:
  0.0 39.4 jit_solution(17588167238129697010)
XLA Ops:
  0.6 0.8 %reshape.9.slots_ref = s32[2,80]{1,0:T(2,128)S(1)} reshape(s32[160]{0:T(256)} %param.10) | data formatting | bytes 1280 | tf_op jit(solution)/shard_map/reshape | solution.py:378
  1.4 0.0 copy-start
  1.4 1.2 %copy-done = bf16[2,2,256,512]{3,2,1,0:T(8,128)(2,1)S(1)} copy-done((bf16[2,2,256,512]{3,2,1,0:T(8,128)(2,1)S(1)}, bf16[2,2,256,512]{3,2,1,0:T(8,128)(2,1)}, u32[]{:S(2)}) %copy-start) | copy-done | bytes 1048600
  2.6 0.0 copy-start.1
  2.6 1.0 %copy-done.1 = bf16[2,256,480]{2,1,0:T(8,128)(2,1)S(1)} copy-done((bf16[2,256,480]{2,1,0:T(8,128)(2,1)S(1)}, bf16[2,256,480]{2,1,0:T(8,128)(2,1)}, u32[]{:S(2)}) %copy-start.1) | copy-done | bytes 491544
  3.7 0.0 copy-start.2
  3.7 1.0 %copy-done.2 = bf16[2,256,512]{2,1,0:T(8,128)(2,1)S(1)} copy-done((bf16[2,256,512]{2,1,0:T(8,128)(2,1)S(1)}, bf16[2,256,512]{2,1,0:T(8,128)(2,1)}, u32[]{:S(2)}) %copy-start.2) | copy-done | bytes 524312
  4.7 0.0 copy-start.3
  4.7 1.0 %copy-done.3 = bf16[2,512,256]{2,1,0:T(8,128)(2,1)S(1)} copy-done((bf16[2,512,256]{2,1,0:T(8,128)(2,1)S(1)}, bf16[2,512,256]{2,1,0:T(8,128)(2,1)}, u32[]{:S(2)}) %copy-start.3) | copy-done | bytes 524312
  5.7 0.0 copy-start.4
  5.7 1.0 %copy-done.4 = f32[240,480]{1,0:T(8,128)S(1)} copy-done((f32[240,480]{1,0:T(8,128)S(1)}, f32[240,480]{1,0:T(8,128)}, u32[]{:S(2)}) %copy-start.4) | copy-done | bytes 460824
  6.8 0.0 copy-start.5
  6.8 0.9 %copy-done.5 = s32[160,128]{1,0:T(8,128)S(1)} copy-done((s32[160,128]{1,0:T(8,128)S(1)}, s32[160,128]{1,0:T(8,128)}, u32[]{:S(2)}) %copy-start.5) | copy-done | bytes 81944
  7.7 0.0 copy-start.6
  7.7 0.8 %copy-done.6 = bf16[2,1,80,128]{3,2,1,0:T(8,128)(2,1)S(1)} copy-done((bf16[2,1,80,128]{3,2,1,0:T(8,128)(2,1)S(1)}, bf16[2,1,80,128]{3,2,1,0:T(8,128)(2,1)}, u32[]{:S(2)}) %copy-start.6) | copy-done | bytes 40984
  8.4 29.1 %shard_map.103 = (bf16[2,1,80,128]{3,2,1,0:T(8,128)(2,1)S(1)}, f32[2,16,16]{2,1,0:T(8,128)S(1)}, f32[2,16,16]{2,1,0:T(8,128)S(1)}) custom-call(bf16[2,1,80,128]{3,2,1,0:T(8,128)(2,1)S(1)} %copy-done.6, s32[2,80]{1,0:T(2,128)S(1)} %reshape.9.slots_ref, s32[160,128]{1,0:T(8,128)S(1)} %copy-done.5, f32[240,480]{1,0:T(8,128)S(1)} %copy-done.4, ...), custom_call_target="tpu_custom_call" | custom-call | tf_op jit(solution)/shard_map/pallas_call | solution.py:342
  37.6 0.6 %copy.14 = bf16[2,1,80,128]{3,2,1,0:T(8,128)(2,1)} copy(bf16[2,1,80,128]{3,2,1,0:T(8,128)(2,1)S(1)} %get-tuple-element.6) | data formatting | bytes 81920
  38.2 0.6 %copy.15 = f32[2,16,16]{2,1,0:T(8,128)} copy(f32[2,16,16]{2,1,0:T(8,128)S(1)} %get-tuple-element.7) | data formatting | bytes 4096
  38.8 0.6 %copy.16 = f32[2,16,16]{2,1,0:T(8,128)} copy(f32[2,16,16]{2,1,0:T(8,128)S(1)} %get-tuple-element.8) | data formatting | bytes 4096
Async XLA Ops:
  1.4 1.2 %copy-start = (bf16[2,2,256,512]{3,2,1,0:T(8,128)(2,1)S(1)}, bf16[2,2,256,512]{3,2,1,0:T(8,128)(2,1)}, u32[]{:S(2)}) copy-start(bf16[2,2,256,512]{3,2,1,0:T(8,128)(2,1)} %constant.8.clone.tz_hbm) | copy-start | bytes 3145732
  2.6 1.0 %copy-start.1 = (bf16[2,256,480]{2,1,0:T(8,128)(2,1)S(1)}, bf16[2,256,480]{2,1,0:T(8,128)(2,1)}, u32[]{:S(2)}) copy-start(bf16[2,256,480]{2,1,0:T(8,128)(2,1)} %constant.11.clone.tr_hbm) | copy-start | bytes 1474564
  3.7 1.0 %copy-start.2 = (bf16[2,256,512]{2,1,0:T(8,128)(2,1)S(1)}, bf16[2,256,512]{2,1,0:T(8,128)(2,1)}, u32[]{:S(2)}) copy-start(bf16[2,256,512]{2,1,0:T(8,128)(2,1)} %constant.10.clone.ty_hbm) | copy-start | bytes 1572868
  4.7 1.0 %copy-start.3 = (bf16[2,512,256]{2,1,0:T(8,128)(2,1)S(1)}, bf16[2,512,256]{2,1,0:T(8,128)(2,1)}, u32[]{:S(2)}) copy-start(bf16[2,512,256]{2,1,0:T(8,128)(2,1)} %constant.9.clone.tx_hbm) | copy-start | bytes 1572868
  5.7 1.0 %copy-start.4 = (f32[240,480]{1,0:T(8,128)S(1)}, f32[240,480]{1,0:T(8,128)}, u32[]{:S(2)}) copy-start(f32[240,480]{1,0:T(8,128)} %pot_hbm.1) | copy-start | bytes 1382404
  6.8 0.9 %copy-start.5 = (s32[160,128]{1,0:T(8,128)S(1)}, s32[160,128]{1,0:T(8,128)}, u32[]{:S(2)}) copy-start(s32[160,128]{1,0:T(8,128)} %entries_ref.1) | copy-start | bytes 245764
  7.7 0.8 %copy-start.6 = (bf16[2,1,80,128]{3,2,1,0:T(8,128)(2,1)S(1)}, bf16[2,1,80,128]{3,2,1,0:T(8,128)(2,1)}, u32[]{:S(2)}) copy-start(bf16[2,1,80,128]{3,2,1,0:T(8,128)(2,1)} %orb_ref.1) | copy-start | bytes 122884

commit v2 on v1

--- a/solution.py
+++ b/solution.py
@@ -75,9 +75,9 @@
     groups,
     points,
     radius,
-    orb_ref,
-    slots_ref,
-    entries_ref,
+    orb_hbm,
+    slots_hbm,
+    entries_hbm,
     pot_hbm,
     tz_hbm,
     tx_hbm,
@@ -86,6 +86,9 @@
     out_ref,
     corr_ref,
     red_ref,
+    orb_ref,
+    slots_ref,
+    entries_ref,
     tz,
     tx,
     ty,
@@ -112,9 +115,10 @@
     band = lax.axis_index("band")
     ga = lax.axis_index("ga")
     total = bands * groups
+    half = bands // 2
     me = ga * bands + band
-    slots = orb_ref.shape[2]
-    width = orb_ref.shape[3]
+    slots = orb_hbm.shape[2]
+    width = orb_hbm.shape[3]
     planes = pot_hbm.shape[0]
     plane_pad = pot.shape[0]
     coarse = ty.shape[2] // 2
@@ -131,6 +135,15 @@
             barrier, inc=1, device_id=where_is(lax.rem(me + k, total)), device_id_type=MESH
         )
 
+    first = [
+        pltpu.make_async_copy(
+            entries_hbm.at[pl.ds(pl.multiple_of(ga * slots, 8), slots)], entries_ref, load_sem.at[5]
+        ),
+        pltpu.make_async_copy(orb_hbm, orb_ref, load_sem.at[6]),
+        pltpu.make_async_copy(slots_hbm, slots_ref, load_sem.at[7]),
+    ]
+    for load in first:
+        load.start()
     loads = [
         pltpu.make_async_copy(pot_hbm, pot.at[pl.ds(0, planes)], load_sem.at[0]),
         pltpu.make_async_copy(tr_hbm, tr, load_sem.at[1]),
@@ -147,7 +160,11 @@
 
     sums[...] = jnp.zeros_like(sums)
 
-    own = entries_ref[pl.ds(pl.multiple_of(ga * slots, 8), slots), :]
+    for load in first:
+        load.wait()
+    own = entries_ref[...]
+    all_sticks = slots_ref[...].reshape(1, groups * slots)
+    sticks = [all_sticks[:, g * slots : (g + 1) * slots] for g in range(groups)]
     lane = lax.broadcasted_iota(jnp.int32, (slots, width), 1)
     inverse = jnp.full((slots, width), -1, jnp.int32)
     for k in range(width):
@@ -176,15 +193,15 @@
 
     def gather_copy(k):
         return pltpu.make_async_remote_copy(
-            src_ref=orb_ref.at[:, 0],
-            dst_ref=gather.at[band],
+            src_ref=orb_hbm.at[:, 0],
+            dst_ref=gather.at[k],
             send_sem=g_send.at[k],
             recv_sem=g_recv.at[k],
             device_id=(lax.rem(band + k, bands), ga),
             device_id_type=MESH,
         )
 
-    @pl.loop(1, bands)
+    @pl.loop(1, half + 1)
     def _(k):
         gather_copy(k).start()
 
@@ -198,7 +215,7 @@
     dense = jnp.zeros((width, 2 * width), F32)
     sub = lax.broadcasted_iota(jnp.int32, (width, slots), 0)
     for g in range(groups):
-        choose = jnp.where(sub == slots_ref[g : g + 1, :], 1.0, 0.0).astype(BF16)
+        choose = jnp.where(sub == sticks[g], 1.0, 0.0).astype(BF16)
         dense += dot(choose, spread[g])
     dense = dense.astype(BF16)
 
@@ -226,7 +243,10 @@
     )
 
     def stick_column(g):
-        row = slots_ref[pl.ds(g, 1), :].astype(F32)
+        row = sticks[0]
+        for other in range(1, groups):
+            row = jnp.where(g == other, sticks[other], row)
+        row = row.astype(F32)
         return jnp.sum(jnp.where(eye, row, 0.0), axis=1, keepdims=True)
 
     lane_f = lane.astype(F32)
@@ -255,26 +275,27 @@
     kinetic = (gx * gx + gz * gz) * (1.0 / float(radius * radius))
     own_index = jnp.maximum(own, 0)
 
-    gather[band] = orb_ref[:, 0]
-
-    @pl.loop(1, bands)
-    def _(k):
-        gather_copy(k).wait()
-
+    gather[0] = orb_ref[:, 0]
     m_re = jnp.where(present, re, 0.0)
     m_im = jnp.where(present, im, 0.0)
 
-    def add_products(first, right_re, right_im):
-        @pl.loop(0, bands)
-        def _(b):
-            left_re = gather[b, 0].astype(F32)
-            left_im = gather[b, 1].astype(F32)
+    def add_products(first, right_re, right_im, fresh):
+        @pl.loop(0, half + 1)
+        def _(k):
+            if fresh:
+                @pl.when(k > 0)
+                def _():
+                    gather_copy(k).wait()
+
+            b = lax.rem(band - k + bands, bands)
+            left_re = gather[k, 0].astype(F32)
+            left_im = gather[k, 1].astype(F32)
             real = left_re * right_re + left_im * right_im
             imag = left_re * right_im - left_im * right_re
             sums[pl.ds(first * bands + b, 1), :] = jnp.sum(real, axis=0, keepdims=True)
             sums[pl.ds((first + 1) * bands + b, 1), :] = jnp.sum(imag, axis=0, keepdims=True)
 
-    add_products(0, m_re, m_im)
+    add_products(0, m_re, m_im, True)
 
     for copy in p_copies:
         copy.wait()
@@ -286,7 +307,7 @@
     h_im = jnp.where(present, kinetic * im + a_im, 0.0).astype(BF16)
     out_ref[0, 0] = h_re
     out_ref[1, 0] = h_im
-    add_products(2, h_re.astype(F32), h_im.astype(F32))
+    add_products(2, h_re.astype(F32), h_im.astype(F32), False)
 
     ones = jnp.full((8, width), 1.0 / float(4 * radius * radius), F32)
     row = lax.dot_general(
@@ -320,9 +341,18 @@
     turned = lax.dot_general(
         unit, rows, NT, preferred_element_type=F32, precision=lax.Precision.HIGHEST
     )
-    for c in range(2):
-        corr_ref[c] = turned[c * bands : (c + 1) * bands]
-        red_ref[c] = turned[(c + 2) * bands : (c + 3) * bands]
+    place_i = lax.broadcasted_iota(jnp.int32, (bands, bands), 0)
+    place_j = lax.broadcasted_iota(jnp.int32, (bands, bands), 1)
+    direct = lax.rem(place_j - place_i + bands, bands) <= half
+
+    def assemble(c, sign):
+        part_of = slice(c * bands, (c + 1) * bands)
+        return jnp.where(direct, turned[part_of], sign * rows[:, part_of])
+
+    corr_ref[0] = assemble(0, 1.0)
+    corr_ref[1] = assemble(1, -1.0)
+    red_ref[0] = assemble(2, 1.0)
+    red_ref[1] = assemble(3, -1.0)
 
 
 def body(bands, groups, orbitals, potential, slot_sticks, stick_entries):
@@ -336,7 +366,7 @@
     sum_rows = -(-4 * bands // 128) * 128
     tz, tx, ty, tr = tables(points, width, radius, groups, planes, plane_pad, coarse)
     vmem = pl.BlockSpec(memory_space=pltpu.VMEM)
-    hbm = pl.BlockSpec(memory_space=pl.ANY)
+    hbm = pl.BlockSpec(memory_space=pltpu.HBM)
     total = bands * groups
     dma = pltpu.SemaphoreType.DMA
     return pl.pallas_call(
@@ -346,9 +376,12 @@
             jax.ShapeDtypeStruct((2, bands, bands), F32),
             jax.ShapeDtypeStruct((2, bands, bands), F32),
         ),
-        in_specs=[vmem, vmem, vmem, hbm, hbm, hbm, hbm, hbm],
+        in_specs=[hbm] * 8,
         out_specs=(vmem, vmem, vmem),
         scratch_shapes=[
+            pltpu.VMEM(orbitals.shape, BF16),
+            pltpu.VMEM(slot_sticks.shape, jnp.int32),
+            pltpu.VMEM((slots, width), jnp.int32),
             pltpu.VMEM(tz.shape[1:], BF16),
             pltpu.VMEM(tx.shape, BF16),
             pltpu.VMEM(ty.shape, BF16),
@@ -358,24 +391,24 @@
             pltpu.VMEM((2, 2 * width, plane_pad), BF16),
             pltpu.VMEM((groups - 1, slots, 2 * width), F32),
             pltpu.VMEM((groups - 1, slots, 2 * width), F32),
-            pltpu.VMEM((bands, 2, slots, width), BF16),
+            pltpu.VMEM((bands // 2 + 1, 2, slots, width), BF16),
             pltpu.VMEM((sum_rows, width), F32),
             pltpu.VMEM((1, sum_rows), F32),
             pltpu.VMEM((total, 1, sum_rows), F32),
-            dma((5,)),
+            dma((8,)),
             dma((groups - 1,)),
             dma((groups - 1,)),
             dma((groups - 1,)),
             dma((groups - 1,)),
-            dma((bands,)),
-            dma((bands,)),
+            dma((bands // 2 + 1,)),
+            dma((bands // 2 + 1,)),
             dma,
             dma,
         ],
         compiler_params=pltpu.CompilerParams(
-            collective_id=0, has_side_effects=True, vmem_limit_bytes=48 * 1024 * 1024
+            collective_id=0, has_side_effects=True, vmem_limit_bytes=67043328 - 81920
         ),
-    )(orbitals, slot_sticks.reshape(groups, slots), stick_entries, potential, tz, tx, ty, tr)
+    )(orbitals, slot_sticks, stick_entries, potential, tz, tx, ty, tr)
 
 
 def solution(mesh):

time: 39.9 us -> 28.2 us (0.71)
  local copies, waits for them, and re-layouts: 9.63 us -> 2.74 us
  Pallas kernels: 29.1 us -> 24.6 us
    unnamed x17 -> x7, local copies, waits for them, and re-layouts: 8.87 us -> 2.74 us
    pallas_call x1, Pallas kernels: 29.1 us -> 24.6 us  [body(): pl.pallas_call(functools.partial(kernel, bands, groups, points, radius),...]
    reshape x1 -> x0, local copies, waits for them, and re-layouts: 0.76 us -> none  [body(): slot_sticks.reshape(groups, slots)]
where the time goes in v2:
time: 28.2 us; the launch traced here: 28 us
  Pallas kernels  24.6 us (87%)
  local copies, waits for them, and re-layouts  2.74 us (10%)
  between operations  0.65 us (2%)
    pallas_call x1, Pallas kernels, body(): pl.pallas_call(functools.partial(kernel, bands, groups, points, radius),...  24.6 us
    unnamed x7, local copies, waits for them, and re-layouts  2.74 us

profile of v2, /device:TPU:0, one launch (start us, length us, event | category | flops | bytes accessed | tf_op | source)
XLA Modules:
  0.0 28.0 jit_solution(11494309542447968509)
XLA Ops:
  0.6 24.6 %shard_map.103 = (bf16[2,1,80,128]{3,2,1,0:T(8,128)(2,1)}, f32[2,16,16]{2,1,0:T(8,128)}, f32[2,16,16]{2,1,0:T(8,128)}) custom-call(bf16[2,1,80,128]{3,2,1,0:T(8,128)(2,1)} %orb_hbm.1, s32[160]{0:T(256)} %slots_hbm.1, s32[160,128]{1,0:T(8,128)} %entries_hbm.1, f32[240,480]{1,0:T(8,128)} %pot_hbm.1, bf16[2,2,256,512]{3,2,1,0:T(8,128)(2,1)} %constant.8.clone.tz_hbm, ...), custom_call_target="tpu_custom_call" | custom-call | tf_op jit(solution)/shard_map/pallas_call | solution.py:372
  25.2 0.0 copy-start.1
  25.2 1.4 %copy.14 = bf16[2,1,80,128]{3,2,1,0:T(8,128)(2,1)} copy(bf16[2,1,80,128]{3,2,1,0:T(8,128)(2,1)} %get-tuple-element.6) | data formatting | bytes 81920
  26.6 0.0 copy-done.1
  26.6 0.0 copy-start
  26.6 0.6 %copy.15 = f32[2,16,16]{2,1,0:T(8,128)} copy(f32[2,16,16]{2,1,0:T(8,128)S(1)} %copy-done.1) | data formatting | bytes 4096
  27.2 0.1 copy-done
  27.3 0.6 %copy.16 = f32[2,16,16]{2,1,0:T(8,128)} copy(f32[2,16,16]{2,1,0:T(8,128)S(1)} %copy-done) | data formatting | bytes 4096
Async XLA Ops:
  25.2 1.4 %copy-start.1 = (f32[2,16,16]{2,1,0:T(8,128)S(1)}, f32[2,16,16]{2,1,0:T(8,128)}, u32[]{:S(2)}) copy-start(f32[2,16,16]{2,1,0:T(8,128)} %get-tuple-element.7) | copy-start | bytes 6148
  26.6 0.7 %copy-start = (f32[2,16,16]{2,1,0:T(8,128)S(1)}, f32[2,16,16]{2,1,0:T(8,128)}, u32[]{:S(2)}) copy-start(f32[2,16,16]{2,1,0:T(8,128)} %get-tuple-element.8) | copy-start | bytes 6148

commit v3 on v2

--- a/solution.py
+++ b/solution.py
@@ -372,9 +372,9 @@
     return pl.pallas_call(
         functools.partial(kernel, bands, groups, points, radius),
         out_shape=(
-            jax.ShapeDtypeStruct(orbitals.shape, BF16),
-            jax.ShapeDtypeStruct((2, bands, bands), F32),
-            jax.ShapeDtypeStruct((2, bands, bands), F32),
+            pltpu.VMEM(orbitals.shape, BF16),
+            pltpu.VMEM((2, bands, bands), F32),
+            pltpu.VMEM((2, bands, bands), F32),
         ),
         in_specs=[hbm] * 8,
         out_specs=(vmem, vmem, vmem),
@@ -406,7 +406,7 @@
             dma,
         ],
         compiler_params=pltpu.CompilerParams(
-            collective_id=0, has_side_effects=True, vmem_limit_bytes=67043328 - 81920
+            collective_id=0, has_side_effects=True, vmem_limit_bytes=60000000
         ),
     )(orbitals, slot_sticks, stick_entries, potential, tz, tx, ty, tr)
 

time: 28.2 us -> 26.7 us (0.947)
  local copies, waits for them, and re-layouts: 2.74 us -> 1.83 us
  Pallas kernels: 24.6 us -> 24 us
    unnamed x7 -> x3, local copies, waits for them, and re-layouts: 2.74 us -> 1.83 us
    pallas_call x1, Pallas kernels: 24.6 us -> 24 us  [body(): pl.pallas_call(functools.partial(kernel, bands, groups, points, radius),...]
where the time goes in v3:
time: 26.7 us; the launch traced here: 26.5 us
  Pallas kernels  24 us (90%)
  local copies, waits for them, and re-layouts  1.83 us (7%)
  between operations  0.64 us (2%)
    pallas_call x1, Pallas kernels, body(): pl.pallas_call(functools.partial(kernel, bands, groups, points, radius),...  24 us
    unnamed x3, local copies, waits for them, and re-layouts  1.83 us

profile of v3, /device:TPU:0, one launch (start us, length us, event | category | flops | bytes accessed | tf_op | source)
XLA Modules:
  0.0 26.5 jit_solution(16356459419194000375)
XLA Ops:
  0.6 24.0 %shard_map.103 = (bf16[2,1,80,128]{3,2,1,0:T(8,128)(2,1)S(1)}, f32[2,16,16]{2,1,0:T(8,128)S(1)}, f32[2,16,16]{2,1,0:T(8,128)S(1)}) custom-call(bf16[2,1,80,128]{3,2,1,0:T(8,128)(2,1)} %orb_hbm.1, s32[160]{0:T(256)} %slots_hbm.1, s32[160,128]{1,0:T(8,128)} %entries_hbm.1, f32[240,480]{1,0:T(8,128)} %pot_hbm.1, bf16[2,2,256,512]{3,2,1,0:T(8,128)(2,1)} %constant.8.clone.tz_hbm, ...), custom_call_target="tpu_custom_call" | custom-call | tf_op jit(solution)/shard_map/pallas_call | solution.py:372
  24.7 0.6 %copy.14 = bf16[2,1,80,128]{3,2,1,0:T(8,128)(2,1)} copy(bf16[2,1,80,128]{3,2,1,0:T(8,128)(2,1)S(1)} %get-tuple-element.3) | data formatting | bytes 81920
  25.3 0.6 %copy.15 = f32[2,16,16]{2,1,0:T(8,128)} copy(f32[2,16,16]{2,1,0:T(8,128)S(1)} %get-tuple-element.4) | data formatting | bytes 4096
  25.9 0.6 %copy.16 = f32[2,16,16]{2,1,0:T(8,128)} copy(f32[2,16,16]{2,1,0:T(8,128)S(1)} %get-tuple-element.5) | data formatting | bytes 4096
